TPU v7x, 128 devices: a whole 4x4x4 slice. The times are simulated.
128 devices in a mesh: expert: 16 (over z, x), tensor: 8 (over y, core).
Axes of the slice: x: 4, y: 4, z: 4, core: 2. Of those that a mesh axis runs over, the one named last changes fastest.
Arguments:
- tokens: bfloat16 [2048, 4096], P('expert'), may hold values from -6 to 6
- scores: float32 [2048, 8], P('expert'), may hold values from -6 to 6
- expert_ids: int32 [2048, 8], P('expert'), may hold values from 0 to 63, all different within a row; in each aligned block of 128 rows (0 to 127, 128 to 255, ...) at most 32 rows name the same one
- gate_weight: bfloat16 [64, 1536, 4096], P('expert', 'tensor'), may hold values from -0.09375 to 0.09375
- up_weight: bfloat16 [64, 1536, 4096], P('expert', 'tensor'), may hold values from -0.09375 to 0.09375
- down_weight: bfloat16 [64, 1536, 4096], P('expert', 'tensor'), may hold values from -0.15625 to 0.15625
Outputs:
- mixed: bfloat16 [2048, 4096], P('expert', 'tensor')
Inputs may be any that keep to these rules, and one draw needn't show every extreme that they name: `expert_ids`: each row names 8 different experts. Among the 128 rows of one owner (rows o * 128 to (o + 1) * 128 - 1) no expert is named more than 32 times.
All inputs are finite; a program needn't handle non-finite values.
Results may differ from a plain program's by a relative error of at most 0.018.
Values may be sent and summed in bfloat16 or wider, within the bound.
A program may use at most 128 MiB of HBM per device.

v0:
```python
import jax
import jax.numpy as jnp
from jax import lax
from jax.sharding import PartitionSpec as P

TOP = 8


def copy_for_each(x, axis):
    copies = jnp.broadcast_to(x, (lax.axis_size(axis), *x.shape))
    return lax.all_to_all(copies, axis, split_axis=0, concat_axis=0, tiled=True)


def in_order(parts, dim):
    dims = list(parts.shape[1:])
    dims[dim] *= parts.shape[0]
    return jnp.moveaxis(parts, 0, dim).reshape(dims)


def gathered_copies(x, axis, dim):
    parts = copy_for_each(x, axis)
    return in_order(parts, dim)


def gate_of(scores):
    lifted = jnp.exp(scores)
    return (lifted / jnp.sum(lifted, axis=-1, keepdims=True)).astype(jnp.bfloat16)


def slot_tables(expert_ids, gate_values, experts, blocks, capacity):
    rows_all = expert_ids.shape[0]
    block_rows = rows_all // blocks
    expert_count = experts.shape[0]
    matches = expert_ids[:, :, None] == experts[None, None, :]
    routed = jnp.any(matches, axis=1).astype(jnp.int32)
    chosen_gate = jnp.sum(
        jnp.where(matches, gate_values.astype(jnp.float32)[:, :, None], jnp.float32(0.0)), axis=1
    )
    folded = routed.reshape(blocks, block_rows, expert_count)
    rank_in_block = jnp.cumsum(folded, axis=1) - folded
    block_start = (jnp.arange(blocks, dtype=jnp.int32) * capacity)[:, None, None]
    slot_index = (block_start + rank_in_block).reshape(rows_all, expert_count)
    slot_index = jnp.where(routed == 1, slot_index, blocks * capacity)
    columns = jnp.broadcast_to(jnp.arange(expert_count, dtype=jnp.int32)[None, :], slot_index.shape)
    position = jnp.broadcast_to(jnp.arange(rows_all, dtype=jnp.int32)[:, None], slot_index.shape)
    slot_token = (
        jnp.full((expert_count, blocks * capacity), rows_all, jnp.int32)
        .at[columns, slot_index]
        .set(position, mode="drop")
    )
    slot_gate = (
        jnp.zeros((expert_count, blocks * capacity), jnp.float32)
        .at[columns, slot_index]
        .set(chosen_gate, mode="drop")
    )
    return (slot_token, slot_gate)


def local(tokens, scores, expert_ids, gate_weight, up_weight, down_weight):
    groups = lax.axis_size("expert")
    ranks = lax.axis_size("tensor")
    local_experts = gate_weight.shape[0]
    owner_rows = tokens.shape[0]
    width = tokens.shape[1]
    share = width // ranks
    capacity = 2 * owner_rows * TOP // (local_experts * groups)
    gate_values = gate_of(scores)
    all_ids = gathered_copies(expert_ids, "expert", 0)
    all_gates = gathered_copies(gate_values, "expert", 0)
    first_expert = lax.axis_index("expert") * local_experts
    held_experts = first_expert + jnp.arange(local_experts, dtype=jnp.int32)
    slot_token, slot_gate = slot_tables(all_ids, all_gates, held_experts, groups, capacity)
    send_order = (
        jnp.arange(local_experts, dtype=jnp.int32)[:, None]
        + local_experts * jnp.arange(groups, dtype=jnp.int32)[None, :]
    ).reshape(-1)
    send_token = slot_tables(expert_ids, gate_values, send_order, 1, capacity)[0]
    send_index = send_token.reshape(-1)
    column_start = lax.axis_index("tensor") * share
    narrow = lax.dynamic_slice_in_dim(tokens, column_start, share, 1)
    outgoing = jnp.take(narrow, send_index, axis=0, mode="fill", fill_value=0).reshape(
        local_experts, groups * capacity, share
    )
    arrived = lax.all_to_all(outgoing, "expert", split_axis=1, concat_axis=1, tiled=True)
    piece = lax.all_gather(arrived, "tensor", axis=2, tiled=True)
    gate_next = jnp.einsum("jcd,jfd->jcf", piece, gate_weight, preferred_element_type=jnp.float32)
    up_next = jnp.einsum("jcd,jfd->jcf", piece, up_weight, preferred_element_type=jnp.float32)
    hidden = (jax.nn.silu(gate_next) * up_next).astype(jnp.bfloat16)
    partial_value = jnp.einsum(
        "jcf,jfd->jcd", hidden, down_weight, preferred_element_type=jnp.float32
    ).astype(jnp.bfloat16)
    summed = lax.psum_scatter(partial_value, "tensor", scatter_dimension=2, tiled=True).astype(
        jnp.float32
    )
    gated = summed * slot_gate[:, :, None]
    returned = lax.all_to_all(
        gated.astype(jnp.bfloat16), "expert", split_axis=1, concat_axis=1, tiled=True
    ).astype(gated.dtype)
    mixed = (
        jnp.zeros((owner_rows, share), jnp.float32)
        .at[send_index]
        .add(returned.reshape(-1, share), mode="drop")
    )
    return mixed.astype(jnp.bfloat16)


def solution(mesh):
    in_specs = (
        P("expert", None),
        P("expert", None),
        P("expert", None),
        P("expert", "tensor", None),
        P("expert", "tensor", None),
        P("expert", "tensor", None),
    )
    out_specs = P("expert", "tensor")
    return jax.shard_map(local, mesh=mesh, in_specs=in_specs, out_specs=out_specs, check_vma=False)
```

profile of v0, /device:TPU:9, one launch (start us, length us, event | category | flops | bytes accessed | tf_op | source)
XLA Modules:
  0.0 370.6 jit_solution(3893563274801632213)
XLA Ops:
  6.5 0.0 copy-start
  6.5 0.0 all-gather.2.cloned.1.call-start
  6.6 0.1 add.116
  6.6 0.9 compare_reduce_fusion.1
  7.5 4.4 %copy.97 = s32[128,64,1]{2,1,0:T(8,128)} copy(s32[128,64,1]{0,1,2:T(8,128)S(1)} %convert_bitcast_fusion.2) | data formatting | bytes 65536 | tf_op jit(solution)/shard_map/convert_element_type | solution.py:35
  12.0 4.5 %fusion.14 = s32[128,64,1]{2,1,0:T(8,128)} fusion(s32[128,64,1]{2,1,0:T(8,128)} %copy.97), kind=kOutput, calls=%fused_computation.52 | output fusion | flops 1040384 | bytes 65536 | tf_op jit(solution)/shard_map/jit(cumsum)/reduce_window_sum | solution.py:40
  16.5 0.0 copy-start.6
  16.5 3.8 %copy.98 = s32[128,64,1]{0,1,2:T(8,128)S(1)} copy(s32[128,64,1]{2,1,0:T(8,128)} %fusion.14) | data formatting | bytes 65536 | tf_op jit(solution)/shard_map/jit(cumsum)/reduce_window_sum | solution.py:40
  20.2 0.0 copy-done.6
  20.3 0.1 multiply_reduce_fusion.1
  20.3 0.0 copy-done.7
  20.3 0.1 and_reduce_fusion.1
  20.4 0.1 copy.99
  20.5 0.1 reshape.257
  20.6 0.1 reshape.259
  20.7 30.4 %scatter_custom_fusion.1 = s32[2048]{0:T(1024)S(1)} fusion(s32[8192]{0:T(1024)S(1)} %reshape.257, s32[8192]{0:T(1024)S(1)} %reshape.259, s32[]{:T(128)} %constant.17.clone.1), kind=kCustom, calls=%fused_computation.41 | custom fusion | bytes 8196
  51.2 0.1 reshape.229
  51.2 0.1 copy.100
  51.3 0.1 reshape.223
  51.4 0.1 reshape.224
  51.5 0.2 copy.102
  51.7 0.0 copy-done
  51.8 7.5 %gather_fusion = bf16[2048,512]{1,0:T(8,128)(2,1)S(1)} fusion(bf16[128,512]{1,0:T(8,128)(2,1)S(1)} %constant_dynamic-slice_fusion, s32[2048]{0:T(1024)S(1)} %broadcast_clamp_fusion), kind=kCustom, calls=%fused_computation | custom fusion | bytes 4202496 | tf_op jit(solution)/shard_map/jit(_take)/gather | solution.py:81
  59.3 5.2 %copy_select_fusion = bf16[4,512,512]{2,0,1:T(4,128)(2,1)S(1)} fusion(bf16[4,512,512]{2,1,0:T(8,128)(2,1)S(1)} %bitcast.45, pred[4,512]{0,1:T(8,128)(4,1)S(1)} %copy.102), kind=kLoop, calls=%fused_computation.8 | loop fusion | flops 1048576 | bytes 4196352 | tf_op jit(solution)/shard_map/jit(_take)/select_n | solution.py:81
  64.5 34.7 %all_to_all.20 = bf16[4,512,512]{2,0,1:T(4,128)(2,1)S(1)} all-to-all(bf16[4,512,512]{2,0,1:T(4,128)(2,1)S(1)} %copy_select_fusion), channel_id=1, replica_groups=mesh['expert'=16,'tensor'=8] {'expert'}, dimensions={1} | all-to-all | bytes 4194304 | tf_op jit(solution)/shard_map/all_to_all | solution.py:84
  99.2 1.8 copy.104
  101.0 0.0 all-gather.2.cloned.1.call-update
  101.0 0.0 reduce-scatter.2.cloned.1.call-start
  101.0 84.0 %all-gather.2.cloned.1.call-done = bf16[4,512,4096]{2,1,0:T(8,128)(2,1)} async-done(((bf16[4,512,512]{2,1,0:T(8,128)(2,1)}), bf16[4,512,4096]{2,1,0:T(8,128)(2,1)}) %all-gather.2.cloned.1.call-update) | async-done | bytes 16777232 | tf_op jit(solution)/shard_map/all_gather | solution.py:85
  185.0 11.0 %fusion.16 = f32[4,512,192]{1,2,0:T(8,128)S(1)} fusion(bf16[4,512,4096]{2,1,0:T(8,128)(2,1)} %all-gather.2.cloned.1.call-done, bf16[4,192,4096]{2,1,0:T(8,128)(2,1)} %param.9), kind=kOutput, calls=%fused_computation.54 | convolution fusion | flops 3221225472 | bytes 24641536 | tf_op jit(solution)/shard_map/jcd,jfd->jcf/dot_general | solution.py:86
  196.0 21.6 %convolution_convert_fusion = bf16[4,512,4096]{2,1,0:T(8,128)(2,1)} fusion(bf16[4,192,4096]{2,1,0:T(8,128)(2,1)} %param.11, f32[4,512,192]{1,2,0:T(8,128)S(1)} %fusion.16, bf16[4,512,4096]{2,1,0:T(8,128)(2,1)} %all-gather.2.cloned.1.call-done, bf16[4,192,4096]{2,1,0:T(8,128)(2,1)} %param.10), kind=kOutput, calls=%fused_computation.4 | convolution fusion | flops 6453198848 | bytes 47710208 | tf_op jit(solution)/shard_map/jcf,jfd->jcd/dot_general | solution.py:89
  217.7 0.0 reduce-scatter.2.cloned.1.call-update
  217.7 0.7 copy-done.3
  218.4 0.6 broadcast_in_dim.87
  219.0 6.7 %all-to-all-start.2 = ((bf16[16,128,8]{1,2,0:T(8,128)(2,1)}), bf16[16,128,8]{1,2,0:T(8,128)(2,1)S(1)}, u32[]{:S(2)}, u32[]{:S(2)}) async-start(bf16[16,128,8]{1,2,0:T(8,128)(2,1)} %broadcast_in_dim.87), calls=%async_computation.3 | async-start | bytes 65536 | tf_op jit(solution)/shard_map/all_to_all | solution.py:11
  225.7 0.1 broadcast_bitcast_fusion
  225.8 6.4 %all-to-all-done.2 = bf16[16,128,8]{1,2,0:T(8,128)(2,1)S(1)} async-done(((bf16[16,128,8]{1,2,0:T(8,128)(2,1)}), bf16[16,128,8]{1,2,0:T(8,128)(2,1)S(1)}, u32[]{:S(2)}, u32[]{:S(2)}) %all-to-all-start.2) | async-done | bytes 32800 | tf_op jit(solution)/shard_map/all_to_all | solution.py:11
  232.1 0.0 copy-done.2
  232.1 0.6 broadcast_in_dim.85
  232.8 3.5 all-to-all-start.1
  236.3 6.4 %all-to-all-done.1 = s32[16,128,8]{1,2,0:T(8,128)S(1)} async-done(((s32[16,128,8]{1,2,0:T(8,128)}), s32[16,128,8]{1,2,0:T(8,128)S(1)}, u32[]{:S(2)}, u32[]{:S(2)}) %all-to-all-start.1) | async-done | bytes 65568 | tf_op jit(solution)/shard_map/all_to_all | solution.py:11
  242.7 0.2 compare_reduce_fusion
  242.9 0.5 copy.105
  243.5 23.3 %fusion.15 = s32[16,128,4]{2,0,1:T(8,128)S(1)} fusion(s32[16,128,4]{2,0,1:T(8,128)S(1)} %copy.105), kind=kOutput, calls=%fused_computation.53 | output fusion | flops 1040384 | bytes 65536 | tf_op jit(solution)/shard_map/jit(cumsum)/reduce_window_sum | solution.py:40
  266.8 0.4 copy.106
  267.3 0.0 copy-done.5
  267.3 0.1 multiply_reduce_fusion
  267.4 0.0 copy-done.4
  267.4 0.1 and_reduce_fusion
  267.5 0.4 copy.107
  267.9 0.6 reshape.263
  268.5 0.2 fusion.3
  268.7 0.4 copy.108
  269.1 0.6 reshape.265
  269.7 30.4 %scatter_custom_fusion.2 = f32[2048]{0:T(1024)S(1)} fusion(s32[8192]{0:T(1024)S(1)} %reshape.263, f32[8192]{0:T(1024)S(1)} %reshape.265, f32[]{:T(128)} %constant.16.clone.1), kind=kCustom, calls=%fused_computation.39 | custom fusion | bytes 8196
  300.2 9.2 %reduce-scatter.2.cloned.1.call-done = bf16[4,512,512]{2,1,0:T(8,128)(2,1)} async-done(((bf16[4,512,4096]{2,1,0:T(8,128)(2,1)}), bf16[4,512,512]{2,1,0:T(8,128)(2,1)}) %reduce-scatter.2.cloned.1.call-update) | async-done | bytes 2097168 | tf_op jit(solution)/shard_map/reduce_scatter | solution.py:92
  309.3 2.1 multiply_convert_fusion
  311.4 1.6 copy.109
  313.0 0.0 copy-start.1
  313.1 36.7 %all_to_all.21 = bf16[4,512,512]{2,0,1:T(4,128)(2,1)S(1)} all-to-all(bf16[4,512,512]{2,0,1:T(4,128)(2,1)S(1)} %copy.109), channel_id=1, replica_groups=mesh['expert'=16,'tensor'=8] {'expert'}, dimensions={1} | all-to-all | bytes 4194304 | tf_op jit(solution)/shard_map/all_to_all | solution.py:96
  349.8 0.4 copy.110
  350.2 12.9 %scatter_custom_fusion = f32[128,512]{1,0:T(8,128)S(1)} fusion(s32[2048]{0:T(1024)S(1)} %bitcast.52, bf16[2048,512]{1,0:T(8,128)(2,1)S(1)} %bitcast.46, f32[]{:T(128)} %constant.16.clone.1), kind=kCustom, calls=%fused_computation.5 | custom fusion | flops 2097152 | bytes 2359300 | tf_op jit(solution)/shard_map/scatter-add | solution.py:102
  363.1 0.7 convert_element_type.85
  363.8 0.0 copy-done.1
  (28 shorter events, 0.2 us)
Async XLA Ops:
  6.5 45.2 %copy-start = (bf16[128,4096]{1,0:T(8,128)(2,1)S(1)}, bf16[128,4096]{1,0:T(8,128)(2,1)}, u32[]{:S(2)}) copy-start(bf16[128,4096]{1,0:T(8,128)(2,1)} %param.6) | copy-start | bytes 3145732
  6.5 178.5 %all-gather.2.cloned.1.call-start = ((), (), s32[]{:S(2)}) async-start(), calls=%async_computation.5 | async-start | bytes 18874368 | tf_op jit(solution)/shard_map/all_gather | solution.py:85
  16.5 3.8 %copy-start.6 = (s32[2]{0:T(128)S(1)}, s32[2]{0:T(128)}, u32[]{:S(2)}) copy-start(s32[2]{0:T(128)} %constant.68) | copy-start | bytes 28
  16.5 3.9 %copy-start.7 = (s32[2]{0:T(128)S(1)}, s32[2]{0:T(128)}, u32[]{:S(2)}) copy-start(s32[2]{0:T(128)} %constant.71) | copy-start | bytes 28
  101.0 208.4 %reduce-scatter.2.cloned.1.call-start = ((), (), s32[]{:S(2)}) async-start(), calls=%async_computation.6 | async-start | bytes 18874368 | tf_op jit(solution)/shard_map/reduce_scatter | solution.py:92
  217.7 0.7 copy-start.3
  217.7 14.5 %copy-start.2 = (s32[128,8]{0,1:T(8,128)S(1)}, s32[128,8]{0,1:T(8,128)}, u32[]{:S(2)}) copy-start(s32[128,8]{0,1:T(8,128)} %param.8) | copy-start | bytes 12292
  218.3 48.9 %copy-start.5 = (s32[2]{0:T(128)S(1)}, s32[2]{0:T(128)}, u32[]{:S(2)}) copy-start(s32[2]{0:T(128)} %constant.74) | copy-start | bytes 28
  218.3 49.0 %copy-start.4 = (s32[2]{0:T(128)S(1)}, s32[2]{0:T(128)}, u32[]{:S(2)}) copy-start(s32[2]{0:T(128)} %constant.77) | copy-start | bytes 28
  219.0 13.1 %all-to-all-start.2 = ((bf16[16,128,8]{1,2,0:T(8,128)(2,1)}), bf16[16,128,8]{1,2,0:T(8,128)(2,1)S(1)}, u32[]{:S(2)}, u32[]{:S(2)}) async-start(bf16[16,128,8]{1,2,0:T(8,128)(2,1)} %broadcast_in_dim.87), calls=%async_computation.3 | async-start | bytes 65536 | tf_op jit(solution)/shard_map/all_to_all | solution.py:11
  232.8 10.0 %all-to-all-start.1 = ((s32[16,128,8]{1,2,0:T(8,128)}), s32[16,128,8]{1,2,0:T(8,128)S(1)}, u32[]{:S(2)}, u32[]{:S(2)}) async-start(s32[16,128,8]{1,2,0:T(8,128)} %broadcast_in_dim.85), calls=%async_computation.2 | async-start | bytes 131072 | tf_op jit(solution)/shard_map/all_to_all | solution.py:11
  313.0 50.7 %copy-start.1 = (bf16[128,4096]{1,0:T(8,128)(2,1)S(1)}, bf16[128,4096]{1,0:T(8,128)(2,1)}, u32[]{:S(2)}) copy-start(bf16[128,4096]{1,0:T(8,128)(2,1)} %param.6) | copy-start | bytes 3145732
Sparse Core Ops, SparseCore 0:
  101.1 83.8 all-gather.1
  217.8 91.4 reduce-scatter.1
where the time goes:
time: 371 us
  waiting for transfers between devices  106 us (29%)
  local copies, waits for them, and re-layouts  86.3 us (23%)
  blocking collectives  71.4 us (19%)
  other arithmetic  50.3 us (14%)
  matrix products  32.6 us (9%)
  between operations  13.7 us (4%)
  starting transfers between devices  10.2 us (3%)
    all_gather x1, waiting for transfers between devices, local(): piece = lax.all_gather(arrived, 'tensor', axis=2, tiled=True)  84 us
    unnamed x24, local copies, waits for them, and re-layouts  62.8 us
    all_to_all x1, blocking collectives, local(): lax.all_to_all(gated.astype(jnp.bfloat16), 'expert', split_axis=1, concat...  36.7 us
    all_to_all x1, blocking collectives, local(): lax.all_to_all(outgoing, 'expert', split_axis=1, concat_axis=1, tiled=True)  34.7 us
    another operation x2, other arithmetic, slot_tables(): rank_in_block = jnp.cumsum(folded, axis=1) - folded  27.8 us
    dot_general x1, matrix products, local(): jnp.einsum('jcf,jfd->jcd', hidden, down_weight, preferred_element_type=jn...  21.6 us
    scatter-add x1, other arithmetic, local(): mixed = jnp.zeros((owner_rows, share), jnp.float32).at[send_index].add(re...  12.9 us
    all_to_all x2, waiting for transfers between devices, copy_for_each(): return lax.all_to_all(copies, axis, split_axis=0, concat_axis=0, tiled=True)  12.8 us
  transfers between devices with their start and end apart: 4, of which 4 were waited for; matrix products, arithmetic and copies ran while one was open for 16% of the time, Pallas kernels for 0%

commit v1 on v0

--- a/solution.py
+++ b/solution.py
@@ -82,7 +82,10 @@
         local_experts, groups * capacity, share
     )
     arrived = lax.all_to_all(outgoing, "expert", split_axis=1, concat_axis=1, tiled=True)
-    piece = lax.all_gather(arrived, "tensor", axis=2, tiled=True)
+    size = lax.axis_size("tensor")
+    shards = jnp.stack([arrived for _ in range(size)])
+    shards = lax.all_to_all(shards, "tensor", split_axis=0, concat_axis=0)
+    piece = jnp.concatenate(shards, axis=2)
     gate_next = jnp.einsum("jcd,jfd->jcf", piece, gate_weight, preferred_element_type=jnp.float32)
     up_next = jnp.einsum("jcd,jfd->jcf", piece, up_weight, preferred_element_type=jnp.float32)
     hidden = (jax.nn.silu(gate_next) * up_next).astype(jnp.bfloat16)

time: 371 us -> 480 us (1.29)
  blocking collectives: 71.4 us -> 262 us
  waiting for transfers between devices: 106 us -> 21.1 us
  local copies, waits for them, and re-layouts: 86.3 us -> 93.9 us
    all_to_all x0 -> x1, blocking collectives: none -> 191 us  [local(): shards = lax.all_to_all(shards, 'tensor', split_axis=0, concat_axis=0)]
    all_gather x1 -> x0, waiting for transfers between devices: 84 us -> none  [local(): piece = lax.all_gather(arrived, 'tensor', axis=2, tiled=True)]
    reshape x0 -> x1, local copies, waits for them, and re-layouts: none -> 7.31 us  [local(): piece = jnp.concatenate(shards, axis=2)]
    unnamed x24 -> x28, local copies, waits for them, and re-layouts: 62.8 us -> 62.8 us
  transfers between devices with their start and end apart: 4 -> 3, of which waited for: 4 -> 3; matrix products, arithmetic and copies ran while one was open for 16% -> 12% of each run, Pallas kernels for 0% -> 0%
where the time goes in v1:
time: 480 us; the launch traced here: 479 us
  blocking collectives  262 us (55%)
  local copies, waits for them, and re-layouts  93.9 us (20%)
  other arithmetic  50.3 us (10%)
  matrix products  30.8 us (6%)
  waiting for transfers between devices  21.1 us (4%)
  between operations  13.8 us (3%)
  starting transfers between devices  7 us (1%)
    all_to_all x1, blocking collectives, local(): shards = lax.all_to_all(shards, 'tensor', split_axis=0, concat_axis=0)  191 us
    unnamed x28, local copies, waits for them, and re-layouts  62.8 us
    all_to_all x1, blocking collectives, local(): lax.all_to_all(gated.astype(jnp.bfloat16), 'expert', split_axis=1, concat...  36.6 us
    all_to_all x1, blocking collectives, local(): lax.all_to_all(outgoing, 'expert', split_axis=1, concat_axis=1, tiled=True)  34.7 us
    another operation x2, other arithmetic, slot_tables(): rank_in_block = jnp.cumsum(folded, axis=1) - folded  27.8 us
    dot_general x1, matrix products, local(): jnp.einsum('jcf,jfd->jcd', hidden, down_weight, preferred_element_type=jn...  21.6 us
    scatter-add x1, other arithmetic, local(): mixed = jnp.zeros((owner_rows, share), jnp.float32).at[send_index].add(re...  12.9 us
    all_to_all x2, waiting for transfers between devices, copy_for_each(): return lax.all_to_all(copies, axis, split_axis=0, concat_axis=0, tiled=True)  12.7 us
  transfers between devices with their start and end apart: 3, of which 3 were waited for; matrix products, arithmetic and copies ran while one was open for 12% of the time, Pallas kernels for 0%

profile of v1, /device:TPU:9, one launch (start us, length us, event | category | flops | bytes accessed | tf_op | source)
XLA Modules:
  0.0 479.3 jit_solution(4882100054351565070)
XLA Ops:
  6.5 0.0 copy-start
  6.5 0.0 reduce-scatter.2.cloned.1.call-start
  6.6 0.1 add.116
  6.6 0.9 compare_reduce_fusion.1
  7.5 4.4 copy.101
  12.0 4.5 fusion.14
  16.5 3.8 copy.102
  20.2 0.0 copy-done.6
  20.3 0.1 multiply_reduce_fusion.1
  20.3 0.0 copy-done.7
  20.3 0.1 and_reduce_fusion.1
  20.4 0.1 copy.103
  20.5 0.1 reshape.267
  20.6 0.1 reshape.269
  20.7 30.4 %scatter_custom_fusion.1 = s32[2048]{0:T(1024)S(1)} fusion(s32[8192]{0:T(1024)S(1)} %reshape.267, s32[8192]{0:T(1024)S(1)} %reshape.269, s32[]{:T(128)} %constant.17.clone.1), kind=kCustom, calls=%fused_computation.41 | custom fusion | bytes 8196
  51.2 0.1 reshape.239
  51.2 0.1 copy.104
  51.3 0.1 reshape.231
  51.4 0.1 reshape.232
  51.5 0.2 copy.106
  51.7 0.0 copy-done
  51.8 7.5 %gather_fusion = bf16[2048,512]{1,0:T(8,128)(2,1)S(1)} fusion(bf16[128,512]{1,0:T(8,128)(2,1)S(1)} %constant_dynamic-slice_fusion, s32[2048]{0:T(1024)S(1)} %broadcast_clamp_fusion), kind=kCustom, calls=%fused_computation | custom fusion | bytes 4202496 | tf_op jit(solution)/shard_map/jit(_take)/gather | solution.py:81
  59.3 5.2 %copy_select_fusion = bf16[4,512,512]{2,0,1:T(4,128)(2,1)S(1)} fusion(bf16[4,512,512]{2,1,0:T(8,128)(2,1)S(1)} %bitcast.51, pred[4,512]{0,1:T(8,128)(4,1)S(1)} %copy.106), kind=kLoop, calls=%fused_computation.8 | loop fusion | flops 1048576 | bytes 4196352 | tf_op jit(solution)/shard_map/jit(_take)/select_n | solution.py:81
  64.5 34.7 %all_to_all.25 = bf16[4,512,512]{2,0,1:T(4,128)(2,1)S(1)} all-to-all(bf16[4,512,512]{2,0,1:T(4,128)(2,1)S(1)} %copy_select_fusion), channel_id=1, replica_groups=mesh['expert'=16,'tensor'=8] {'expert'}, dimensions={1} | all-to-all | bytes 4194304 | tf_op jit(solution)/shard_map/all_to_all | solution.py:84
  99.2 0.4 copy.108
  99.6 1.6 stack.2
  101.2 0.0 slice-start
  101.2 191.2 %all_to_all.26 = bf16[8,4,512,512]{3,2,1,0:T(8,128)(2,1)S(1)} all-to-all(bf16[8,4,512,512]{3,2,1,0:T(8,128)(2,1)S(1)} %stack.2), channel_id=1, replica_groups=mesh['expert'=16,'tensor'=8] {'tensor'}, dimensions={0} | all-to-all | bytes 33554432 | tf_op jit(solution)/shard_map/all_to_all | solution.py:87
  292.4 7.3 %copy.116 = bf16[8,4,64,8,512]{4,3,0,2,1:T(8,128)(2,1)} copy(bf16[8,4,64,8,512]{4,3,2,1,0:T(8,128)(2,1)S(1)} %bitcast.50) | data formatting | bytes 33554432 | tf_op jit(solution)/shard_map/reshape | solution.py:88
  299.7 0.0 slice-done
  299.7 0.0 slice-done.1
  299.7 9.2 %fusion.16 = f32[4,512,192]{1,2,0:T(8,128)S(1)} fusion(bf16[4,512,4096]{2,1,0:T(8,128)(2,1)} %bitcast.48, bf16[4,192,4096]{2,1,0:T(8,128)(2,1)S(1)} %bitcast.54), kind=kOutput, calls=%fused_computation.54 | convolution fusion | flops 3221225472 | bytes 24641536 | tf_op jit(solution)/shard_map/jcd,jfd->jcf/dot_general | solution.py:89
  309.0 21.6 %convolution_convert_fusion = bf16[4,512,4096]{2,1,0:T(8,128)(2,1)} fusion(bf16[4,192,4096]{2,1,0:T(8,128)(2,1)} %param.11, f32[4,512,192]{1,2,0:T(8,128)S(1)} %fusion.16, bf16[4,512,4096]{2,1,0:T(8,128)(2,1)} %bitcast.49, bf16[4,192,4096]{2,1,0:T(8,128)(2,1)} %param.10), kind=kOutput, calls=%fused_computation.4 | convolution fusion | flops 6453198848 | bytes 47710208 | tf_op jit(solution)/shard_map/jcf,jfd->jcd/dot_general | solution.py:92
  330.6 0.0 reduce-scatter.2.cloned.1.call-update
  330.6 0.7 copy-done.3
  331.3 0.6 broadcast_in_dim.87
  331.9 3.5 all-to-all-start.3
  335.4 0.1 broadcast_bitcast_fusion
  335.5 6.3 %all-to-all-done.3 = bf16[16,128,8]{1,2,0:T(8,128)(2,1)S(1)} async-done(((bf16[16,128,8]{1,2,0:T(8,128)(2,1)}), bf16[16,128,8]{1,2,0:T(8,128)(2,1)S(1)}, u32[]{:S(2)}, u32[]{:S(2)}) %all-to-all-start.3) | async-done | bytes 32800 | tf_op jit(solution)/shard_map/all_to_all | solution.py:11
  341.8 0.0 copy-done.2
  341.8 0.6 broadcast_in_dim.85
  342.5 3.5 all-to-all-start.2
  346.0 6.4 %all-to-all-done.2 = s32[16,128,8]{1,2,0:T(8,128)S(1)} async-done(((s32[16,128,8]{1,2,0:T(8,128)}), s32[16,128,8]{1,2,0:T(8,128)S(1)}, u32[]{:S(2)}, u32[]{:S(2)}) %all-to-all-start.2) | async-done | bytes 65568 | tf_op jit(solution)/shard_map/all_to_all | solution.py:11
  352.4 0.2 compare_reduce_fusion
  352.6 0.5 copy.110
  353.2 23.3 %fusion.15 = s32[16,128,4]{2,0,1:T(8,128)S(1)} fusion(s32[16,128,4]{2,0,1:T(8,128)S(1)} %copy.110), kind=kOutput, calls=%fused_computation.53 | output fusion | flops 1040384 | bytes 65536 | tf_op jit(solution)/shard_map/jit(cumsum)/reduce_window_sum | solution.py:40
  376.5 0.4 copy.111
  377.0 0.0 copy-done.5
  377.0 0.1 multiply_reduce_fusion
  377.1 0.1 and_reduce_fusion
  377.2 0.4 copy.112
  377.6 0.6 reshape.273
  378.2 0.2 fusion.3
  378.4 0.4 copy.113
  378.8 0.6 reshape.275
  379.4 30.4 %scatter_custom_fusion.2 = f32[2048]{0:T(1024)S(1)} fusion(s32[8192]{0:T(1024)S(1)} %reshape.273, f32[8192]{0:T(1024)S(1)} %reshape.275, f32[]{:T(128)} %constant.16.clone.1), kind=kCustom, calls=%fused_computation.39 | custom fusion | bytes 8196
  409.9 8.4 %reduce-scatter.2.cloned.1.call-done = bf16[4,512,512]{2,1,0:T(8,128)(2,1)} async-done(((bf16[4,512,4096]{2,1,0:T(8,128)(2,1)}), bf16[4,512,512]{2,1,0:T(8,128)(2,1)}) %reduce-scatter.2.cloned.1.call-update) | async-done | bytes 2097168 | tf_op jit(solution)/shard_map/reduce_scatter | solution.py:95
  418.2 2.1 multiply_convert_fusion
  420.3 1.6 copy.114
  421.9 0.0 copy-start.1
  421.9 36.6 %all_to_all.27 = bf16[4,512,512]{2,0,1:T(4,128)(2,1)S(1)} all-to-all(bf16[4,512,512]{2,0,1:T(4,128)(2,1)S(1)} %copy.114), channel_id=1, replica_groups=mesh['expert'=16,'tensor'=8] {'expert'}, dimensions={1} | all-to-all | bytes 4194304 | tf_op jit(solution)/shard_map/all_to_all | solution.py:99
  458.5 0.4 copy.115
  458.9 12.9 %scatter_custom_fusion = f32[128,512]{1,0:T(8,128)S(1)} fusion(s32[2048]{0:T(1024)S(1)} %bitcast.60, bf16[2048,512]{1,0:T(8,128)(2,1)S(1)} %bitcast.52, f32[]{:T(128)} %constant.16.clone.1), kind=kCustom, calls=%fused_computation.5 | custom fusion | flops 2097152 | bytes 2359300 | tf_op jit(solution)/shard_map/scatter-add | solution.py:105
  471.8 0.7 convert_element_type.85
  (33 shorter events, 0.2 us)
Async XLA Ops:
  6.5 45.2 %copy-start = (bf16[128,4096]{1,0:T(8,128)(2,1)S(1)}, bf16[128,4096]{1,0:T(8,128)(2,1)}, u32[]{:S(2)}) copy-start(bf16[128,4096]{1,0:T(8,128)(2,1)} %param.6) | copy-start | bytes 3145732
  6.5 411.7 %reduce-scatter.2.cloned.1.call-start = ((), (), s32[]{:S(2)}) async-start(), calls=%async_computation.6 | async-start | bytes 18874368 | tf_op jit(solution)/shard_map/reduce_scatter | solution.py:95
  16.5 3.8 copy-start.6
  16.5 3.9 copy-start.7
  101.2 198.6 %slice-start = ((s8[6291456]{0:T(1024)(128)(4,1)}), s8[2097152]{0:T(1024)(128)(4,1)S(1)}, s32[]{:S(2)}) async-start(s8[6291456]{0:T(1024)(128)(4,1)} %bitcast.53), calls=%async_computation.7 | async-start | bytes 4194304
  292.4 7.3 %slice-start.1 = ((s8[6291456]{0:T(1024)(128)(4,1)}), s8[4194304]{0:T(1024)(128)(4,1)S(1)}, s32[]{:S(2)}) async-start(s8[6291456]{0:T(1024)(128)(4,1)} %bitcast.53), calls=%async_computation.8 | async-start | bytes 8388608
  330.6 0.7 copy-start.3
  330.6 11.2 %copy-start.2 = (s32[128,8]{0,1:T(8,128)S(1)}, s32[128,8]{0,1:T(8,128)}, u32[]{:S(2)}) copy-start(s32[128,8]{0,1:T(8,128)} %param.8) | copy-start | bytes 12292
  331.3 45.7 %copy-start.5 = (s32[2]{0:T(128)S(1)}, s32[2]{0:T(128)}, u32[]{:S(2)}) copy-start(s32[2]{0:T(128)} %constant.74) | copy-start | bytes 28
  331.3 45.8 %copy-start.4 = (s32[2]{0:T(128)S(1)}, s32[2]{0:T(128)}, u32[]{:S(2)}) copy-start(s32[2]{0:T(128)} %constant.77) | copy-start | bytes 28
  331.9 9.9 %all-to-all-start.3 = ((bf16[16,128,8]{1,2,0:T(8,128)(2,1)}), bf16[16,128,8]{1,2,0:T(8,128)(2,1)S(1)}, u32[]{:S(2)}, u32[]{:S(2)}) async-start(bf16[16,128,8]{1,2,0:T(8,128)(2,1)} %broadcast_in_dim.87), calls=%async_computation.4 | async-start | bytes 65536 | tf_op jit(solution)/shard_map/all_to_all | solution.py:11
  342.5 10.0 %all-to-all-start.2 = ((s32[16,128,8]{1,2,0:T(8,128)}), s32[16,128,8]{1,2,0:T(8,128)S(1)}, u32[]{:S(2)}, u32[]{:S(2)}) async-start(s32[16,128,8]{1,2,0:T(8,128)} %broadcast_in_dim.85), calls=%async_computation.3 | async-start | bytes 131072 | tf_op jit(solution)/shard_map/all_to_all | solution.py:11
  421.9 50.6 %copy-start.1 = (bf16[128,4096]{1,0:T(8,128)(2,1)S(1)}, bf16[128,4096]{1,0:T(8,128)(2,1)}, u32[]{:S(2)}) copy-start(bf16[128,4096]{1,0:T(8,128)(2,1)} %param.6) | copy-start | bytes 3145732
Sparse Core Ops, SparseCore 0:
  330.7 87.4 reduce-scatter.1
